TPU v7x, 32 devices: a whole 2x2x4 slice. The times are simulated.
32 devices in a mesh: lat: 4 (over z), lon: 8 (over y, x, core).
Axes of the slice: x: 2, y: 2, z: 4, core: 2. Of those that a mesh axis runs over, the one named last changes fastest.
Arguments:
- fields: float32 [32, 2880, 384], P('lat', 'lon'), may hold values from -6 to 6
- cutoff: int32 [32], P('lat'), may hold values from 1 to 1395, as said below
Outputs:
- filtered: float32 [32, 2880, 384], P('lat', 'lon')
Inputs may be any that keep to these rules, and one draw needn't show every extreme that they name: cutoff[g] lies between 1 and 1 + (1439)(2 p + 1) // 32, where p is the number of rows between row g and the nearer pole; this ceiling grows from the pole rows to the equator.
All inputs are finite; a program needn't handle non-finite values.
Results may differ from a plain program's by a relative error of at most 0.0003.
Values sent between devices are 32-bit elements; how exact they have to be, the bound alone decides.
A program may use at most 64 MiB of HBM per device.

v0:
```python
import functools
import math

import jax
import jax.numpy as jnp
import ml_dtypes
import numpy as np
from jax import lax
from jax.experimental import pallas as pl
from jax.experimental.pallas import tpu as pltpu
from jax.sharding import PartitionSpec as P

RADIX = 8


def split_np(a):
    hi = a.astype(ml_dtypes.bfloat16)
    lo = (a - hi.astype(np.float64)).astype(ml_dtypes.bfloat16)
    return hi, lo


def fourier_table(sub, padded):
    turn = np.outer(np.arange(sub), np.arange(sub)) % sub
    angle = 2.0 * np.pi * turn / sub
    both = np.concatenate([np.cos(angle), np.sin(angle)], axis=0)
    both = np.pad(both, ((0, 0), (0, padded - sub)))
    hi, lo = split_np(both)
    return np.concatenate([hi, lo, hi], axis=1)


def twist_table(sub, length):
    b = np.arange(RADIX // 2 + 1)
    angle = 2.0 * np.pi * np.outer(np.arange(sub), b) / length
    return np.concatenate([np.cos(angle), np.sin(angle)], axis=1).astype(np.float32)


def gain_table(cut, sub, length):
    half = RADIX // 2
    wave = np.arange(sub)[:, None] * RADIX + np.arange(half + 1)[None, :]
    folded = np.minimum(wave, length - wave)
    scale = np.where((np.arange(half + 1) % half) == 0, 1.0, 2.0)[None, :] / length
    inverse_sine = 1.0 / np.sin(np.pi * np.maximum(folded, 1) / length)
    ratio = jnp.sin(cut * jnp.float32(math.pi / length)) * inverse_sine.astype(np.float32)
    gain = jnp.where(folded.astype(np.float32) <= cut, 1.0, ratio * ratio)
    return gain * scale.astype(np.float32)


def three(table, z, padded):
    pad = padded - z.shape[0]
    if pad:
        z = jnp.concatenate([z, jnp.zeros((pad, z.shape[1]), z.dtype)], axis=0)
    hi = z.astype(jnp.bfloat16)
    lo = (z - hi.astype(jnp.float32)).astype(jnp.bfloat16)
    return jnp.dot(table, jnp.concatenate([hi, hi, lo], axis=0), preferred_element_type=jnp.float32)


def filter_kernel(sub, padded, flag_ref, x_ref, table_ref, twist_ref, gain_ref, y_ref):
    width = x_ref.shape[-1]
    half = RADIX // 2
    r = math.sqrt(0.5)

    @pl.when(flag_ref[0] == 0)
    def _():
        y_ref[...] = x_ref[...]

    @pl.when(flag_ref[0] != 0)
    def _():
        x = [x_ref[pl.ds(j * sub, sub), :] for j in range(RADIX)]
        s = [x[j] + x[j + 4] for j in range(4)]
        d = [x[j] - x[j + 4] for j in range(4)]
        s02, s13 = s[0] + s[2], s[1] + s[3]
        p, q = r * (d[1] - d[3]), r * (d[1] + d[3])
        spectra = [
            (s02 + s13, None),
            (d[0] + p, -(d[2] + q)),
            (s[0] - s[2], s[3] - s[1]),
            (d[0] - p, d[2] - q),
            (s02 - s13, None),
        ]
        table = table_ref[...]
        back = []
        for b in range(half + 1):
            re, im = spectra[b]
            gain = gain_ref[:, b : b + 1]
            if b == 0:
                f = three(table, re, padded)
                g = three(table, jnp.concatenate([f[:sub] * gain, f[sub:] * gain], axis=1), padded)
                back.append((g[:sub, :width] + g[sub:, width:], None))
                continue
            c = twist_ref[:, b : b + 1]
            t = twist_ref[:, half + 1 + b : half + 2 + b]
            if im is None:
                zr, zi = re * c, -(re * t)
            else:
                zr, zi = re * c + im * t, im * c - re * t
            f = three(table, jnp.concatenate([zr, zi], axis=1), padded)
            fr = (f[:sub, :width] + f[sub:, width:]) * gain
            fi = (f[:sub, width:] - f[sub:, :width]) * gain
            g = three(table, jnp.concatenate([fr, fi], axis=1), padded)
            gr = g[:sub, :width] - g[sub:, width:]
            gi = g[:sub, width:] + g[sub:, :width]
            back.append((gr * c - gi * t, gr * t + gi * c))
        y0, y4 = back[0][0], back[4][0]
        (a1, b1), (a2, b2), (a3, b3) = back[1:4]
        e, o = y0 + y4, y0 - y4
        u, v = a1 + a3, b1 - b3
        w, z = r * (a1 - a3), r * (b1 + b3)
        outs = {
            0: e + a2 + u,
            4: e + a2 - u,
            2: e - a2 - v,
            6: e - a2 + v,
            1: o - b2 + w - z,
            5: o - b2 - w + z,
            3: o + b2 - w - z,
            7: o + b2 + w + z,
        }
        for j in range(RADIX):
            y_ref[pl.ds(j * sub, sub), :] = outs[j]


def filter_row(row, cut, polar):
    length, channels = row.shape
    sub = length // RADIX
    padded = -(-sub // 128) * 128
    block = 128 if channels % 128 == 0 else channels
    table = fourier_table(sub, padded)
    twist = twist_table(sub, length)
    gain = gain_table(cut, sub, length)
    whole = lambda a: pl.BlockSpec(a.shape, lambda i: (0, 0))
    return pl.pallas_call(
        functools.partial(filter_kernel, sub, padded),
        out_shape=jax.ShapeDtypeStruct(row.shape, row.dtype),
        grid=(channels // block,),
        in_specs=[
            pl.BlockSpec(memory_space=pltpu.SMEM),
            pl.BlockSpec((length, block), lambda i: (0, i)),
            whole(table),
            whole(twist),
            whole(gain),
        ],
        out_specs=pl.BlockSpec((length, block), lambda i: (0, i)),
        compiler_params=pltpu.CompilerParams(vmem_limit_bytes=56 * 1024 * 1024),
        name="row_filter",
    )(polar.reshape(1), row, table, twist, gain)


def polar_table(row_count, band_count):
    total_rows = row_count * band_count
    row_ids = np.arange(total_rows)
    polar_flags = (np.abs(2 * row_ids + 1 - total_rows) * 5 > 2 * total_rows).astype(np.int32)
    return polar_flags.reshape(band_count, row_count)


def local(fields, cutoff):
    rows, segment, channels = fields.shape
    ring = lax.axis_size("lon")
    groups = max(1, ring // rows)
    each = rows * groups // ring
    width = channels // groups
    assert each * ring == rows * groups and width * groups == channels
    pieces = fields
    if groups > 1:
        pieces = fields.reshape(rows, segment, groups, width).transpose(0, 2, 1, 3)
    pieces = pieces.reshape(ring, each, segment, width)
    whole = lax.all_to_all(pieces, "lon", 0, 0, tiled=True)
    first_row = lax.axis_index("lon") * each // groups
    flags = jnp.asarray(polar_table(rows, lax.axis_size("lat")))[lax.axis_index("lat")]
    done = []
    for i in range(each):
        row = whole[:, i].reshape(ring * segment, width)
        cut = lax.dynamic_index_in_dim(cutoff, first_row + i, 0, False).astype(jnp.float32)
        flag = lax.dynamic_index_in_dim(flags, first_row + i, 0, False)
        done.append(filter_row(row, cut, flag).reshape(ring, segment, width))
    back = lax.all_to_all(jnp.stack(done, axis=1), "lon", 0, 0, tiled=True)
    if groups > 1:
        back = back.reshape(rows, groups, segment, width).transpose(0, 2, 1, 3)
    return back.reshape(rows, segment, channels)


def solution(mesh):
    return jax.shard_map(
        local,
        mesh=mesh,
        in_specs=(P("lat", "lon", None), P("lat")),
        out_specs=P("lat", "lon", None),
        check_vma=False,
    )
```

profile of v0, /device:TPU:0, one launch (start us, length us, event | category | flops | bytes accessed | tf_op | source)
XLA Modules:
  0.0 136.2 jit_solution(16394941703821263636)
XLA Ops:
  0.0 0.0 copy-start.3
  0.0 0.0 copy-start
  0.0 0.0 copy-start.1
  0.0 0.0 copy-start.2
  0.0 5.4 %all-to-all-start = ((f32[8,1,360,384]{3,2,1,0:T(8,128)}), f32[8,1,360,384]{3,2,1,0:T(8,128)}, u32[]{:S(2)}, u32[]{:S(2)}) async-start(f32[8,1,360,384]{3,2,1,0:T(8,128)} %bitcast.10), calls=%async_computation | async-start | bytes 8847360 | tf_op jit(solution)/shard_map/all_to_all | solution.py:166
  5.4 0.0 copy-done.3
  5.4 0.6 dynamic_slice.12
  6.7 1.2 dynamic_slice.10
  7.9 0.0 copy-done
  7.9 0.0 copy-done.1
  7.9 0.0 copy-done.2
  7.9 0.7 fusion.gain_ref
  8.7 48.4 %all-to-all-done = f32[8,1,360,384]{3,2,1,0:T(8,128)} async-done(((f32[8,1,360,384]{3,2,1,0:T(8,128)}), f32[8,1,360,384]{3,2,1,0:T(8,128)}, u32[]{:S(2)}, u32[]{:S(2)}) %all-to-all-start) | async-done | bytes 4423712 | tf_op jit(solution)/shard_map/all_to_all | solution.py:166
  57.0 22.0 %row_filter.1 = f32[2880,384]{1,0:T(8,128)} custom-call(s32[1]{0:T(128)} %bitcast.flag_ref, f32[2880,384]{1,0:T(8,128)} %bitcast.2.x_ref, bf16[720,1152]{1,0:T(8,128)(2,1)} %constant.63.clone.table_ref, f32[360,10]{1,0:T(8,128)} %constant.64.clone.twist_ref, f32[360,5]{1,0:T(8,128)} %fusion.gain_ref), custom_call_target="tpu_custom_call" | custom-call | tf_op jit(solution)/shard_map/row_filter/pallas_call | solution.py:131
  79.0 55.1 %all_to_all.10 = f32[8,1,360,384]{3,2,1,0:T(8,128)S(1)} all-to-all(f32[8,1,360,384]{3,2,1,0:T(8,128)} %bitcast.8), channel_id=1, replica_groups=mesh['lat'=4,'lon'=8] {'lon'}, dimensions={0} | all-to-all | bytes 8847360 | tf_op jit(solution)/shard_map/all_to_all | solution.py:175
  134.1 2.1 %copy.11 = f32[8,360,384]{2,1,0:T(8,128)} copy(f32[8,360,384]{2,1,0:T(8,128)S(1)} %bitcast.9) | data formatting | bytes 8847360
Async XLA Ops:
  0.0 5.4 %copy-start.3 = (s32[8]{0:T(128)S(1)}, s32[8]{0:T(128)}, u32[]{:S(2)}) copy-start(s32[8]{0:T(128)} %param.9) | copy-start | bytes 100
  0.0 7.9 %copy-start = (f32[360,5]{1,0:T(8,128)S(1)}, f32[360,5]{1,0:T(8,128)}, u32[]{:S(2)}) copy-start(f32[360,5]{1,0:T(8,128)} %constant.65) | copy-start | bytes 21604
  0.0 7.9 %copy-start.1 = (f32[360,5]{1,0:T(8,128)S(1)}, f32[360,5]{1,0:T(8,128)}, u32[]{:S(2)}) copy-start(f32[360,5]{1,0:T(8,128)} %constant.61.clone) | copy-start | bytes 21604
  0.0 7.9 %copy-start.2 = (f32[5]{0:T(128)S(1)}, f32[5]{0:T(128)}, u32[]{:S(2)}) copy-start(f32[5]{0:T(128)} %constant.66) | copy-start | bytes 64
  0.0 57.0 %all-to-all-start = ((f32[8,1,360,384]{3,2,1,0:T(8,128)}), f32[8,1,360,384]{3,2,1,0:T(8,128)}, u32[]{:S(2)}, u32[]{:S(2)}) async-start(f32[8,1,360,384]{3,2,1,0:T(8,128)} %bitcast.10), calls=%async_computation | async-start | bytes 8847360 | tf_op jit(solution)/shard_map/all_to_all | solution.py:166
where the time goes:
time: 137 us; the launch traced here: 136 us
  blocking collectives  55.1 us (40%)
  waiting for transfers between devices  48.4 us (35%)
  Pallas kernels  22 us (16%)
  starting transfers between devices  5.36 us (4%)
  local copies, waits for them, and re-layouts  3.93 us (3%)
    all_to_all x1, blocking collectives, local(): back = lax.all_to_all(jnp.stack(done, axis=1), 'lon', 0, 0, tiled=True)  55.1 us
    all_to_all x1, waiting for transfers between devices, local(): whole = lax.all_to_all(pieces, 'lon', 0, 0, tiled=True)  48.4 us
    pallas_call x1, Pallas kernels, filter_row(): pl.pallas_call(functools.partial(filter_kernel, sub, padded), out_shape=j...  22 us
    all_to_all x1, starting transfers between devices, local(): whole = lax.all_to_all(pieces, 'lon', 0, 0, tiled=True)  5.36 us
  transfers between devices with their start and end apart: 1, of which 1 were waited for; matrix products, arithmetic and copies ran while one was open for 2% of the time, Pallas kernels for 0%

commit v1 on v0

v1 whole, which is shorter than its diff:
```python
import functools
import math

import jax
import jax.numpy as jnp
import ml_dtypes
import numpy as np
from jax import lax
from jax.experimental import pallas as pl
from jax.experimental.pallas import tpu as pltpu
from jax.sharding import PartitionSpec as P

RADIX = 8


def split_np(a):
    hi = a.astype(ml_dtypes.bfloat16)
    lo = (a - hi.astype(np.float64)).astype(ml_dtypes.bfloat16)
    return hi, lo


def fourier_table(sub, padded):
    turn = np.outer(np.arange(sub), np.arange(sub)) % sub
    angle = 2.0 * np.pi * turn / sub
    both = np.concatenate([np.cos(angle), np.sin(angle)], axis=0)
    both = np.pad(both, ((0, 0), (0, padded - sub)))
    hi, lo = split_np(both)
    return np.concatenate([hi, lo, hi], axis=1)


def twist_table(sub, length):
    b = np.arange(RADIX // 2 + 1)
    angle = 2.0 * np.pi * np.outer(np.arange(sub), b) / length
    return np.concatenate([np.cos(angle), np.sin(angle)], axis=1).astype(np.float32)


def gain_table(cut, sub, length):
    half = RADIX // 2
    wave = np.arange(sub)[:, None] * RADIX + np.arange(half + 1)[None, :]
    folded = np.minimum(wave, length - wave)
    scale = np.where((np.arange(half + 1) % half) == 0, 1.0, 2.0)[None, :] / length
    inverse_sine = 1.0 / np.sin(np.pi * np.maximum(folded, 1) / length)
    ratio = jnp.sin(cut * jnp.float32(math.pi / length)) * inverse_sine.astype(np.float32)
    gain = jnp.where(folded.astype(np.float32) <= cut, 1.0, ratio * ratio)
    return gain * scale.astype(np.float32)


def three(table, z, padded):
    pad = padded - z.shape[0]
    if pad:
        z = jnp.concatenate([z, jnp.zeros((pad, z.shape[1]), z.dtype)], axis=0)
    hi = z.astype(jnp.bfloat16)
    lo = (z - hi.astype(jnp.float32)).astype(jnp.bfloat16)
    return jnp.dot(table, jnp.concatenate([hi, hi, lo], axis=0), preferred_element_type=jnp.float32)


def filter_row(sub, padded, x_ref, table_ref, twist_ref, gains, y_ref):
    width = x_ref.shape[-1]
    half = RADIX // 2
    r = math.sqrt(0.5)
    x = [x_ref[pl.ds(j * sub, sub), :] for j in range(RADIX)]
    s = [x[j] + x[j + 4] for j in range(4)]
    d = [x[j] - x[j + 4] for j in range(4)]
    s02, s13 = s[0] + s[2], s[1] + s[3]
    p, q = r * (d[1] - d[3]), r * (d[1] + d[3])
    spectra = [
        (s02 + s13, None),
        (d[0] + p, -(d[2] + q)),
        (s[0] - s[2], s[3] - s[1]),
        (d[0] - p, d[2] - q),
        (s02 - s13, None),
    ]
    table = table_ref[...]
    back = []
    for b in range(half + 1):
        re, im = spectra[b]
        gain = gains[:, b : b + 1]
        if b == 0:
            f = three(table, re, padded)
            g = three(table, jnp.concatenate([f[:sub] * gain, f[sub:] * gain], axis=1), padded)
            back.append((g[:sub, :width] + g[sub:, width:], None))
            continue
        c = twist_ref[:, b : b + 1]
        t = twist_ref[:, half + 1 + b : half + 2 + b]
        if im is None:
            zr, zi = re * c, -(re * t)
        else:
            zr, zi = re * c + im * t, im * c - re * t
        f = three(table, jnp.concatenate([zr, zi], axis=1), padded)
        fr = (f[:sub, :width] + f[sub:, width:]) * gain
        fi = (f[:sub, width:] - f[sub:, :width]) * gain
        g = three(table, jnp.concatenate([fr, fi], axis=1), padded)
        gr = g[:sub, :width] - g[sub:, width:]
        gi = g[:sub, width:] + g[sub:, :width]
        back.append((gr * c - gi * t, gr * t + gi * c))
    y0, y4 = back[0][0], back[4][0]
    (a1, b1), (a2, b2), (a3, b3) = back[1:4]
    e, o = y0 + y4, y0 - y4
    u, v = a1 + a3, b1 - b3
    w, z = r * (a1 - a3), r * (b1 + b3)
    outs = {
        0: e + a2 + u,
        4: e + a2 - u,
        2: e - a2 - v,
        6: e - a2 + v,
        1: o - b2 + w - z,
        5: o - b2 - w + z,
        3: o + b2 - w - z,
        7: o + b2 + w + z,
    }
    for j in range(RADIX):
        y_ref[pl.ds(j * sub, sub), :] = outs[j]


def split_table(a):
    hi = a.astype(jnp.bfloat16)
    lo = (a - hi.astype(jnp.float32)).astype(jnp.bfloat16)
    return jnp.concatenate([hi, lo, hi], axis=1)


def snap(a):
    return (np.round(a * 2.0**22) / 2.0**22).astype(np.float32)


def toeplitz(symbol, sub):
    line = np.fft.ifft(symbol).real
    index = np.arange(sub)
    return line[(index[:, None] - index[None, :]) % symbol.shape[0]]


class Plan:
    def __init__(self, rows, segment, channels, ring, bands):
        length, total = segment * ring, rows * bands
        self.width = 128 if channels % 128 == 0 else channels
        blocks = channels // self.width
        row_ids = np.arange(total)
        polar = np.abs(2 * row_ids + 1 - total) * 5 > 2 * total
        poles = np.minimum(row_ids, total - 1 - row_ids)
        count = int(poles[polar].max()) + 1
        cuts = 1 + (length // 2 - 1) * (2 * np.arange(count) + 1) // total
        full = -(-segment // 8) * 8
        ranks = [min(full, -(-((2 * int(c) + 1) // ring + 21) // 8) * 8) for c in cuts]
        self.rank = max(ranks)
        self.rank_pad = -(-self.rank // 128) * 128
        self.sub_pad = -(-segment // 128) * 128
        wave = np.arange(length)
        folded = np.minimum(wave, length - wave)
        sine = np.sin(np.pi * np.maximum(folded, 1) / length) ** 2
        spot = np.arange(segment)
        probe = np.cos(1.0 + 0.37 * spot * spot)
        self.basis = np.zeros((count, segment, self.rank_pad), np.float32)
        self.basis_t = np.zeros((count, self.rank, self.sub_pad), np.float32)
        self.rest = np.zeros((count, segment, self.sub_pad), np.float32)
        top = np.sin(np.pi * cuts / length) ** 2
        self.top = top.astype(np.float32)
        for p in range(count):
            take = min(ranks[p], segment)
            side = spot[1:] * (segment - spot[1:]) / 2.0
            band = (cuts[p] + 0.5) / length
            tri = np.diag(((segment - 1) / 2.0 - spot) ** 2 * np.cos(2.0 * np.pi * band))
            tri = tri + np.diag(side, 1) + np.diag(side, -1)
            vectors = np.linalg.eigh(tri)[1][:, ::-1][:, :take]
            vectors = vectors * np.where(probe @ vectors < 0, -1.0, 1.0)
            basis = snap(vectors)
            if take == segment:
                basis = np.eye(segment, dtype=np.float32)
            self.basis[p, :, :take] = basis
            self.basis_t[p, :take, :segment] = basis.T
            near = toeplitz(np.minimum(1.0 / sine, 1.0 / top[p]) * top[p], segment)
            wide = basis.astype(np.float64)
            self.rest[p, :, :segment] = snap(near - wide @ (wide.T @ near @ wide) @ wide.T)
        slots = -(-rows * blocks // ring)
        self.slots = slots
        self.row_pole = np.zeros((bands, rows), np.int32)
        self.row_on = np.zeros((bands, rows), np.int32)
        self.dest = np.zeros((bands, rows, blocks), np.int32)
        self.offset = np.zeros((bands, rows, blocks), np.int32)
        self.unit_row = np.zeros((bands, ring, slots), np.int32)
        self.unit_pole = np.zeros((bands, ring, slots), np.int32)
        self.unit_on = np.zeros((bands, ring, slots), np.int32)
        self.unit_offset = np.zeros((bands, ring, slots), np.int32)
        self.height = 8
        for b in range(bands):
            ids = np.arange(rows) + b * rows
            self.row_on[b] = polar[ids]
            self.row_pole[b] = np.where(polar[ids], poles[ids], 0)
            held = [[] for _ in range(ring)]
            load = [0] * ring
            units = [(ranks[poles[ids[i]]], i, c) for i in range(rows) if polar[ids[i]] for c in range(blocks)]
            for rank, i, c in sorted(units, key=lambda u: (-u[0], u[1], u[2])):
                d = min((e for e in range(ring) if len(held[e]) < slots), key=lambda e: (load[e], e))
                held[d].append((i, c, rank))
                load[d] += rank
            self.height = max(self.height, max(load))
            for d in range(ring):
                start = 0
                for n, (i, c, rank) in enumerate(sorted(held[d])):
                    self.dest[b, i, c], self.offset[b, i, c] = d, start
                    self.unit_row[b, d, n], self.unit_on[b, d, n] = i, 1
                    self.unit_pole[b, d, n], self.unit_offset[b, d, n] = poles[ids[i]], start
                    start += rank


def pack_kernel(plan, pole, on, dest, offset, x_ref, basis_ref, out_ref, hold):
    i = pl.program_id(0)
    width, blocks = plan.width, dest.shape[0] // on.shape[0]

    @pl.when(i == 0)
    def _():
        hold[...] = jnp.zeros_like(hold)

    @pl.when(on[i] != 0)
    def _():
        z = three(split_table(basis_ref[0]), x_ref[0], plan.sub_pad)
        for c in range(blocks):
            at = pl.multiple_of(offset[i * blocks + c], 8)
            hold[dest[i * blocks + c], pl.ds(at, plan.rank), :] = z[:, c * width : (c + 1) * width]

    @pl.when(i == pl.num_programs(0) - 1)
    def _():
        out_ref[...] = hold[:, : plan.height, :]


def unit_kernel(plan, sub, padded, pole, on, offset, w_ref, basis_ref, basis_t_ref, table_ref, twist_ref, gain_ref, out_ref, came, hold, x_row, y_row):
    i = pl.program_id(0)
    ring, width = w_ref.shape[0], plan.width
    segment = basis_ref.shape[1]

    @pl.when(i == 0)
    def _():
        hold[...] = jnp.zeros_like(hold)
        came[:, : plan.height, :] = w_ref[...]
        came[:, plan.height :, :] = jnp.zeros((ring, plan.rank, width), jnp.float32)

    @pl.when(on[i] != 0)
    def _():
        at = pl.multiple_of(offset[i], 8)
        z = jnp.concatenate([came[j, pl.ds(at, plan.rank), :] for j in range(ring)], axis=1)
        x = three(split_table(basis_ref[0]), z, plan.rank_pad)
        for j in range(ring):
            x_row[pl.ds(j * segment, segment), :] = x[:, j * width : (j + 1) * width]
        filter_row(sub, padded, x_row, table_ref, twist_ref, gain_ref[0], y_row)
        y = jnp.concatenate([y_row[pl.ds(j * segment, segment), :] for j in range(ring)], axis=1)
        z = three(split_table(basis_t_ref[0]), y, plan.sub_pad)
        for j in range(ring):
            hold[j, pl.ds(at, plan.rank), :] = z[:, j * width : (j + 1) * width]

    @pl.when(i == pl.num_programs(0) - 1)
    def _():
        out_ref[...] = hold[:, : plan.height, :]


def unpack_kernel(plan, pole, on, dest, offset, w_ref, x_ref, scale_ref, basis_ref, rest_ref, y_ref, came):
    i = pl.program_id(0)
    ring, width = w_ref.shape[0], plan.width
    blocks = dest.shape[0] // on.shape[0]

    @pl.when(i == 0)
    def _():
        came[:, : plan.height, :] = w_ref[...]
        came[:, plan.height :, :] = jnp.zeros((ring, plan.rank, width), jnp.float32)

    @pl.when(on[i] == 0)
    def _():
        y_ref[...] = x_ref[...]

    @pl.when(on[i] != 0)
    def _():
        parts = []
        for c in range(blocks):
            at = pl.multiple_of(offset[i * blocks + c], 8)
            parts.append(came[dest[i * blocks + c], pl.ds(at, plan.rank), :])
        coef = jnp.concatenate(parts, axis=1)
        low = three(split_table(basis_ref[0]), coef, plan.rank_pad)
        high = three(split_table(rest_ref[0]), x_ref[0], plan.sub_pad)
        y_ref[0] = low + high * scale_ref[i]


def local(ring, bands, fields, cutoff):
    rows, segment, channels = fields.shape
    length = ring * segment
    sub = length // RADIX
    padded = -(-sub // 128) * 128
    plan = Plan(rows, segment, channels, ring, bands)
    width, height, rank = plan.width, plan.height, plan.rank
    band, me = lax.axis_index("lat"), lax.axis_index("lon")
    params = pltpu.CompilerParams(vmem_limit_bytes=56 * 1024 * 1024)
    f32 = jnp.float32

    pick = lambda a, *at: functools.reduce(lambda t, n: lax.dynamic_index_in_dim(t, n, 0, False), at, jnp.asarray(a))
    pole, on = pick(plan.row_pole, band), pick(plan.row_on, band)
    dest, offset = pick(plan.dest, band).reshape(-1), pick(plan.offset, band).reshape(-1)
    unit_row, unit_on = pick(plan.unit_row, band, me), pick(plan.unit_on, band, me)
    unit_pole, unit_offset = pick(plan.unit_pole, band, me), pick(plan.unit_offset, band, me)
    cut = cutoff.astype(f32)
    scale = jnp.sin(cut * f32(math.pi / length)) ** 2 / jnp.asarray(plan.top)[pole]
    gains = jnp.stack([gain_table(cut[unit_row[n]], sub, length) for n in range(plan.slots)])

    by_row = pl.BlockSpec((1, segment, channels), lambda i, *s: (i, 0, 0))
    by_pole = lambda a: pl.BlockSpec((1,) + a.shape[1:], lambda i, pole, *s: (pole[i], 0, 0))
    whole = lambda a: pl.BlockSpec(a.shape, lambda i, *s: (0,) * a.ndim)
    sent = jax.ShapeDtypeStruct((ring, height, width), f32)
    buffer = pltpu.VMEM((ring, height + rank, width), f32)

    packed = pl.pallas_call(
        functools.partial(pack_kernel, plan),
        out_shape=sent,
        grid_spec=pltpu.PrefetchScalarGridSpec(
            num_scalar_prefetch=4,
            grid=(rows,),
            in_specs=[by_row, by_pole(plan.basis_t)],
            out_specs=whole(sent),
            scratch_shapes=[buffer],
        ),
        compiler_params=params,
        name="pack",
    )(pole, on, dest, offset, fields, plan.basis_t)
    packed = lax.all_to_all(packed, "lon", 0, 0, tiled=True)
    table = fourier_table(sub, padded)
    twist = twist_table(sub, length)
    packed = pl.pallas_call(
        functools.partial(unit_kernel, plan, sub, padded),
        out_shape=sent,
        grid_spec=pltpu.PrefetchScalarGridSpec(
            num_scalar_prefetch=3,
            grid=(plan.slots,),
            in_specs=[
                whole(sent),
                by_pole(plan.basis),
                by_pole(plan.basis_t),
                whole(table),
                whole(twist),
                pl.BlockSpec((1,) + gains.shape[1:], lambda i, *s: (i, 0, 0)),
            ],
            out_specs=whole(sent),
            scratch_shapes=[buffer, buffer, pltpu.VMEM((length, width), f32), pltpu.VMEM((length, width), f32)],
        ),
        compiler_params=params,
        name="unit_filter",
    )(unit_pole, unit_on, unit_offset, packed, plan.basis, plan.basis_t, table, twist, gains)
    packed = lax.all_to_all(packed, "lon", 0, 0, tiled=True)
    return pl.pallas_call(
        functools.partial(unpack_kernel, plan),
        out_shape=jax.ShapeDtypeStruct(fields.shape, fields.dtype),
        grid_spec=pltpu.PrefetchScalarGridSpec(
            num_scalar_prefetch=4,
            grid=(rows,),
            in_specs=[
                whole(sent),
                by_row,
                pl.BlockSpec(memory_space=pltpu.SMEM),
                by_pole(plan.basis),
                by_pole(plan.rest),
            ],
            out_specs=by_row,
            scratch_shapes=[buffer],
        ),
        compiler_params=params,
        name="unpack",
    )(pole, on, dest, offset, packed, fields, scale, plan.basis, plan.rest)


def solution(mesh):
    return jax.shard_map(
        functools.partial(local, mesh.shape["lon"], mesh.shape["lat"]),
        mesh=mesh,
        in_specs=(P("lat", "lon", None), P("lat")),
        out_specs=P("lat", "lon", None),
        check_vma=False,
    )
```

time: 137 us -> 104 us (0.76)
  blocking collectives: 55.1 us -> 0 us
  Pallas kernels: 22 us -> 50.2 us
  waiting for transfers between devices: 48.4 us -> 22.1 us
  between operations: 0.75 us -> 7.77 us
  local copies, waits for them, and re-layouts: 3.93 us -> 10.5 us
  other arithmetic: 0.71 us -> 4.13 us
  starting transfers between devices: 5.36 us -> 8.77 us
    all_to_all x1 -> x0, blocking collectives: 55.1 us -> none  [local(): back = lax.all_to_all(jnp.stack(done, axis=1), 'lon', 0, 0, tiled=True)]
    pallas_call x1 -> x3, Pallas kernels: 22 us -> 50.2 us  [the longest x1 27.2 us: local(): pl.pallas_call(functools.partial(unit_kernel, plan, sub, padded), out_sha...]
    all_to_all x1 -> x2, waiting for transfers between devices: 48.4 us -> 22.1 us  [local(): packed = lax.all_to_all(packed, 'lon', 0, 0, tiled=True)]
    squeeze x0 -> x3, local copies, waits for them, and re-layouts: none -> 3.75 us  [local(): lax.dynamic_index_in_dim(t, n, 0, False)]
    all_to_all x1 -> x2, starting transfers between devices: 5.36 us -> 8.77 us  [local(): packed = lax.all_to_all(packed, 'lon', 0, 0, tiled=True)]
    another operation x0 -> x2, other arithmetic: none -> 2.8 us  [local(): jnp.stack([gain_table(cut[unit_row[n]], sub, length) for n in range(plan....]
  transfers between devices with their start and end apart: 1 -> 2, of which waited for: 1 -> 2; matrix products, arithmetic and copies ran while one was open for 2% -> 9% of each run, Pallas kernels for 0% -> 0%
where the time goes in v1:
time: 104 us
  Pallas kernels  50.2 us (48%)
  waiting for transfers between devices  22.1 us (21%)
  local copies, waits for them, and re-layouts  10.5 us (10%)
  starting transfers between devices  8.77 us (8%)
  between operations  7.77 us (7%)
  other arithmetic  4.13 us (4%)
    pallas_call x1, Pallas kernels, local(): pl.pallas_call(functools.partial(unit_kernel, plan, sub, padded), out_sha...  27.2 us
    all_to_all x2, waiting for transfers between devices, local(): packed = lax.all_to_all(packed, 'lon', 0, 0, tiled=True)  22.1 us
    pallas_call x1, Pallas kernels, local(): pl.pallas_call(functools.partial(unpack_kernel, plan), out_shape=jax.Shap...  13.5 us
    pallas_call x1, Pallas kernels, local(): pl.pallas_call(functools.partial(pack_kernel, plan), out_shape=sent, grid...  9.52 us
    all_to_all x2, starting transfers between devices, local(): packed = lax.all_to_all(packed, 'lon', 0, 0, tiled=True)  8.77 us
    squeeze x3, local copies, waits for them, and re-layouts, local(): lax.dynamic_index_in_dim(t, n, 0, False)  3.75 us
    another operation x2, other arithmetic, local(): jnp.stack([gain_table(cut[unit_row[n]], sub, length) for n in range(plan....  2.8 us
    unnamed x14, local copies, waits for them, and re-layouts  2.22 us
  transfers between devices with their start and end apart: 2, of which 2 were waited for; matrix products, arithmetic and copies ran while one was open for 9% of the time, Pallas kernels for 0%

profile of v1, /device:TPU:0, one launch (start us, length us, event | category | flops | bytes accessed | tf_op | source)
XLA Modules:
  0.0 103.5 jit_solution(17195011946533482726)
XLA Ops:
  0.0 0.7 constant_dynamic-slice_fusion.4
  0.7 0.6 reshape.51.offset
  1.3 0.6 reshape.50.dest
  1.9 1.3 %fusion.6 = (s32[8]{0:T(128)}, s32[8]{0:T(128)}) fusion(s32[4,8]{1,0:T(4,128)} %constant.152.clone, s32[]{:T(128)S(6)} %select_n.52, s32[4,8]{1,0:T(4,128)} %constant.151.clone), kind=kLoop, calls=%fused_computation.21 | loop fusion | bytes 132 | tf_op jit(solution)/shard_map/jit(dynamic_index_in_dim)/squeeze | solution.py:290
  3.2 0.0 copy-start.6
  3.2 0.0 copy-start.3
  3.2 0.0 copy-start.4
  3.2 0.0 copy-start.5
  3.2 9.5 %pack.1 = f32[8,352,128]{2,1,0:T(8,128)} custom-call(s32[8]{0:T(128)} %get-tuple-element.17.pole, s32[8]{0:T(128)} %get-tuple-element.16.on, s32[24]{0:T(128)} %reshape.50.dest, s32[24]{0:T(128)} %reshape.51.offset, f32[8,360,384]{2,1,0:T(8,128)} %x_ref.3, f32[10,240,384]{2,1,0:T(8,128)} %constant.163.clone.basis_ref.basis_t_ref), custom_call_target="tpu_custom_call" | custom-call | tf_op jit(solution)/shard_map/pack/pallas_call | solution.py:305
  12.7 5.2 %all-to-all-start = ((f32[8,352,128]{2,1,0:T(8,128)}), f32[8,352,128]{2,1,0:T(8,128)S(1)}, u32[]{:S(2)}, u32[]{:S(2)}) async-start(f32[8,352,128]{2,1,0:T(8,128)} %pack.1), calls=%async_computation | async-start | bytes 2883584 | tf_op jit(solution)/shard_map/all_to_all | solution.py:318
  17.9 0.7 constant_dynamic-slice_fusion
  18.6 0.7 fusion.13
  23.0 0.0 copy-done.6
  24.9 0.7 fusion.12
  27.7 1.2 %fusion.9.offset = s32[3]{0:T(128)} fusion(s32[4,8,3]{2,1,0:T(8,128)} %constant.158.clone, s32[]{:T(128)S(6)} %select_n.53, s32[]{:T(128)S(6)} %select_n.55), kind=kLoop, calls=%fused_computation.24 | loop fusion | bytes 32 | tf_op jit(solution)/shard_map/jit(dynamic_index_in_dim)/squeeze | solution.py:290
  28.9 1.2 %fusion.7 = (s32[3]{0:T(128)}, s32[3]{0:T(128)}) fusion(s32[4,8,3]{2,1,0:T(8,128)} %constant.157.clone, s32[]{:T(128)S(6)} %select_n.53, s32[]{:T(128)S(6)} %select_n.55, s32[4,8,3]{2,1,0:T(8,128)} %constant.156.clone), kind=kLoop, calls=%fused_computation.22 | loop fusion | bytes 56 | tf_op jit(solution)/shard_map/jit(dynamic_index_in_dim)/squeeze | solution.py:290
  30.1 0.0 copy-done.3
  30.1 0.0 copy-done.4
  30.1 0.0 copy-done.5
  30.1 1.9 %fusion.5 = (f32[1,360,5]{2,1,0:T(8,128)S(1)}, f32[1,360,5]{2,1,0:T(8,128)S(1)}, f32[1,360,5]{2,1,0:T(8,128)S(1)}) fusion(f32[360,5]{1,0:T(8,128)S(1)} %copy-done.3, f32[360,5]{1,0:T(8,128)S(1)} %copy-done.4, f32[]{:T(128)S(6)} %multiply.9, f32[5]{0:T(128)S(1)} %copy-done.5, f32[]{:T(128)} %bitcast.6, f32[]{:T(128)S(6)} %multiply.11, f32[]{:T(128)} %bitcast.12, ...), kind=kLoop, calls=%fused_computation.10 | loop fusion | flops 21600 | bytes 36044 | tf_op jit(solution)/shard_map/stack | solution.py:297
  32.1 0.9 pad_maximum_fusion.gain_ref
  32.9 4.5 %all-to-all-done.w_ref = f32[8,352,128]{2,1,0:T(8,128)S(1)} async-done(((f32[8,352,128]{2,1,0:T(8,128)}), f32[8,352,128]{2,1,0:T(8,128)S(1)}, u32[]{:S(2)}, u32[]{:S(2)}) %all-to-all-start) | async-done | bytes 1441824 | tf_op jit(solution)/shard_map/all_to_all | solution.py:318
  37.5 1.1 %copy-done.1 = f32[8,352,128]{2,1,0:T(8,128)} copy-done((f32[8,352,128]{2,1,0:T(8,128)}, f32[8,352,128]{2,1,0:T(8,128)S(1)}, u32[]{:S(2)}) %copy-start.1) | copy-done | bytes 1441816
  38.6 27.2 %unit_filter.1 = f32[8,352,128]{2,1,0:T(8,128)} custom-call(s32[3]{0:T(128)} %get-tuple-element.18.pole, s32[3]{0:T(128)} %get-tuple-element.19.on, s32[3]{0:T(128)} %fusion.9.offset, f32[8,352,128]{2,1,0:T(8,128)} %copy-done.1, f32[10,360,256]{2,1,0:T(8,128)} %constant.164.clone.basis_ref, f32[10,240,384]{2,1,0:T(8,128)} %constant.163.clone.basis_ref.basis_t_ref, ...), custom_call_target="tpu_custom_call" | custom-call | tf_op jit(solution)/shard_map/unit_filter/pallas_call | solution.py:321
  65.8 3.6 %all-to-all-start.1 = ((f32[8,352,128]{2,1,0:T(8,128)}), f32[8,352,128]{2,1,0:T(8,128)S(1)}, u32[]{:S(2)}, u32[]{:S(2)}) async-start(f32[8,352,128]{2,1,0:T(8,128)} %unit_filter.1), calls=%async_computation.1 | async-start | bytes 2883584 | tf_op jit(solution)/shard_map/all_to_all | solution.py:341
  69.4 0.7 fusion.10
  70.1 0.0 copy-done
  70.1 0.6 gather_fusion
  70.7 0.6 multiply_divide_fusion.scale_ref
  71.4 17.5 %all-to-all-done.1.w_ref = f32[8,352,128]{2,1,0:T(8,128)S(1)} async-done(((f32[8,352,128]{2,1,0:T(8,128)}), f32[8,352,128]{2,1,0:T(8,128)S(1)}, u32[]{:S(2)}, u32[]{:S(2)}) %all-to-all-start.1) | async-done | bytes 1441824 | tf_op jit(solution)/shard_map/all_to_all | solution.py:341
  88.9 1.1 %copy-done.2 = f32[8,352,128]{2,1,0:T(8,128)} copy-done((f32[8,352,128]{2,1,0:T(8,128)}, f32[8,352,128]{2,1,0:T(8,128)S(1)}, u32[]{:S(2)}) %copy-start.2) | copy-done | bytes 1441816
  90.0 13.5 %unpack.1 = f32[8,360,384]{2,1,0:T(8,128)} custom-call(s32[8]{0:T(128)} %get-tuple-element.17.pole, s32[8]{0:T(128)} %get-tuple-element.16.on, s32[24]{0:T(128)} %reshape.50.dest, s32[24]{0:T(128)} %reshape.51.offset, f32[8,352,128]{2,1,0:T(8,128)} %copy-done.2, f32[8,360,384]{2,1,0:T(8,128)} %x_ref.3, f32[8]{0:T(128)} %multiply_divide_fusion.scale_ref, ...), custom_call_target="tpu_custom_call" | custom-call | tf_op jit(solution)/shard_map/unpack/pallas_call | solution.py:342
  (5 shorter events, 0.0 us)
Async XLA Ops:
  3.2 19.8 %copy-start.6 = (s32[8]{0:T(128)S(1)}, s32[8]{0:T(128)}, u32[]{:S(2)}) copy-start(s32[8]{0:T(128)} %param.26) | copy-start | bytes 100
  3.2 27.0 %copy-start.3 = (f32[360,5]{1,0:T(8,128)S(1)}, f32[360,5]{1,0:T(8,128)}, u32[]{:S(2)}) copy-start(f32[360,5]{1,0:T(8,128)} %constant.168) | copy-start | bytes 21604
  3.2 27.0 %copy-start.4 = (f32[360,5]{1,0:T(8,128)S(1)}, f32[360,5]{1,0:T(8,128)}, u32[]{:S(2)}) copy-start(f32[360,5]{1,0:T(8,128)} %constant.161.clone) | copy-start | bytes 21604
  3.2 27.0 %copy-start.5 = (f32[5]{0:T(128)S(1)}, f32[5]{0:T(128)}, u32[]{:S(2)}) copy-start(f32[5]{0:T(128)} %constant.169) | copy-start | bytes 64
  12.7 24.8 %all-to-all-start = ((f32[8,352,128]{2,1,0:T(8,128)}), f32[8,352,128]{2,1,0:T(8,128)S(1)}, u32[]{:S(2)}, u32[]{:S(2)}) async-start(f32[8,352,128]{2,1,0:T(8,128)} %pack.1), calls=%async_computation | async-start | bytes 2883584 | tf_op jit(solution)/shard_map/all_to_all | solution.py:318
  37.5 1.1 %copy-start.1 = (f32[8,352,128]{2,1,0:T(8,128)}, f32[8,352,128]{2,1,0:T(8,128)S(1)}, u32[]{:S(2)}) copy-start(f32[8,352,128]{2,1,0:T(8,128)S(1)} %all-to-all-done.w_ref) | copy-start | bytes 4325380
  38.6 31.5 %copy-start = (f32[10]{0:T(128)S(1)}, f32[10]{0:T(128)}, u32[]{:S(2)}) copy-start(f32[10]{0:T(128)} %constant.159.clone) | copy-start | bytes 124
  65.8 23.1 %all-to-all-start.1 = ((f32[8,352,128]{2,1,0:T(8,128)}), f32[8,352,128]{2,1,0:T(8,128)S(1)}, u32[]{:S(2)}, u32[]{:S(2)}) async-start(f32[8,352,128]{2,1,0:T(8,128)} %unit_filter.1), calls=%async_computation.1 | async-start | bytes 2883584 | tf_op jit(solution)/shard_map/all_to_all | solution.py:341
  88.9 1.1 %copy-start.2 = (f32[8,352,128]{2,1,0:T(8,128)}, f32[8,352,128]{2,1,0:T(8,128)S(1)}, u32[]{:S(2)}) copy-start(f32[8,352,128]{2,1,0:T(8,128)S(1)} %all-to-all-done.1.w_ref) | copy-start | bytes 4325380
